TPU v7x, 32 devices: a whole 2x2x4 slice. The times are simulated.
32 devices in a mesh: wide: 8 (over z, y), narrow: 4 (over x, core).
Axes of the slice: x: 2, y: 2, z: 4, core: 2. Of those that a mesh axis runs over, the one named last changes fastest.
Arguments:
- values: float32 [512, 16384], P(('wide', 'narrow')), may hold values from -200 to 200, as said below
- cloud_words: int32 [512, 512], P(('wide', 'narrow')), may hold values from -2147483648 to 2147483647, as said below
- history_len: int32 [1], replicated, may hold values from 96 to 256
- monitor_start: int32 [1], replicated, may hold values from 256 to 384
- boundary_table: int32 [512], replicated, may hold values from 500 to 2000
Outputs:
- ratio: float32 [512, 16384], P(('wide', 'narrow'))
- peak_so_far: float32 [512, 16384], P(('wide', 'narrow'))
Inputs may be any that keep to these rules, and one draw needn't show every extreme that they name: `values`: values of an index series, mixed noise and a seasonal cycle of varying scale. `cloud_words`: bit b of word j in the row of date t is 1 when pixel 32 j + b is clear at date t; the first 16 dates are clear for every pixel.
All inputs are finite; a program needn't handle non-finite values.
Results may differ from a plain program's by a relative error of at most 0.0003.
Values sent between devices are 32-bit elements; how exact they have to be, the bound alone decides.
No kernel may reach another device: no remote copies, remote signals or barrier semaphores. Data moves between devices by JAX's collectives and lax.ppermute only.
A program may use at most 64 MiB of HBM per device.

v0:
```python
import math

import jax
import jax.numpy as jnp
from jax import lax
from jax.sharding import PartitionSpec as P

PERIOD = 46
HARMONICS = 3
COLS = 8
WINDOW = 64


HIGH = lax.Precision.HIGHEST


def unpack_clear(words):
    shifts = jnp.arange(32, dtype=jnp.int32)
    flags = jnp.bitwise_and(jnp.right_shift(words[:, :, None], shifts[None, None, :]), jnp.int32(1))
    return flags.reshape(words.shape[0], words.shape[1] * 32).astype(jnp.float32)


def harmonic_design(dates):
    day_float = jnp.arange(dates, dtype=jnp.int32).astype(jnp.float32)
    columns = [jnp.ones((dates,), jnp.float32), day_float / dates]
    for harmonic in range(1, HARMONICS + 1):
        phases = 2.0 * math.pi * harmonic / PERIOD * day_float
        columns.append(jnp.cos(phases))
        columns.append(jnp.sin(phases))
    return jnp.stack(columns, axis=1)


def solve_batched(normal_mat, target):
    size_cols = normal_mat.shape[0]
    factor = [[None] * size_cols for row_idx in range(size_cols)]
    for row_idx in range(size_cols):
        for col_idx in range(row_idx + 1):
            summed = normal_mat[row_idx, col_idx]
            for mid_idx in range(col_idx):
                summed = summed - factor[row_idx][mid_idx] * factor[col_idx][mid_idx]
            if row_idx == col_idx:
                factor[row_idx][col_idx] = jnp.sqrt(summed)
            else:
                factor[row_idx][col_idx] = summed / factor[col_idx][col_idx]
    forward = []
    for row_idx in range(size_cols):
        summed = target[row_idx]
        for mid_idx in range(row_idx):
            summed = summed - factor[row_idx][mid_idx] * forward[mid_idx]
        forward.append(summed / factor[row_idx][row_idx])
    solution = [None] * size_cols
    for row_idx in reversed(range(size_cols)):
        summed = forward[row_idx]
        for mid_idx in range(row_idx + 1, size_cols):
            summed = summed - factor[mid_idx][row_idx] * solution[mid_idx]
        solution[row_idx] = summed / factor[row_idx][row_idx]
    return jnp.stack(solution, axis=0)


def fit_statistic(values, clear, history_len, monitor_start, boundary_table):
    dates = values.shape[0]
    day = jnp.arange(dates, dtype=jnp.int32)
    design = harmonic_design(dates)
    in_history = (day < history_len[0]).astype(jnp.float32)[:, None]
    weight = clear * in_history
    outer = (design[:, :, None] * design[:, None, :]).reshape(dates, COLS * COLS)
    normal_mat = jnp.dot(
        outer.T, weight, precision=HIGH, preferred_element_type=jnp.float32
    ).reshape(COLS, COLS, -1)
    target = jnp.dot(design.T, weight * values, precision=HIGH, preferred_element_type=jnp.float32)
    coeffs = solve_batched(normal_mat, target)
    fitted = jnp.dot(design, coeffs, precision=HIGH, preferred_element_type=jnp.float32)
    resid = clear * (values - fitted)
    count = jnp.sum(weight, axis=0)
    squares = jnp.sum(weight * resid * resid, axis=0)
    sigma = jnp.sqrt(squares / (count - COLS) + 1e-06)
    lagged = day[:, None] - day[None, :]
    banded = ((lagged >= 0) & (lagged < WINDOW)).astype(jnp.float32)
    moving = jnp.dot(banded, resid, precision=HIGH, preferred_element_type=jnp.float32)
    scaled = moving / (sigma * jnp.sqrt(count))[None, :]
    bounds = boundary_table.astype(jnp.float32) * 0.001
    watching = (day >= monitor_start[0])[:, None]
    return jnp.where(watching, scaled / bounds[:, None], jnp.float32(0.0))


def per_device(values, cloud_words, history_len, monitor_start, boundary_table):
    arrived = lax.all_to_all(values, ("wide", "narrow"), split_axis=1, concat_axis=0, tiled=True)
    words = lax.all_to_all(cloud_words, ("wide", "narrow"), split_axis=1, concat_axis=0, tiled=True)
    ratio = fit_statistic(arrived, unpack_clear(words), history_len, monitor_start, boundary_table)
    outgoing = jnp.stack([ratio, lax.cummax(jnp.abs(ratio), axis=0)])
    returned = lax.all_to_all(outgoing, ("wide", "narrow"), split_axis=1, concat_axis=2, tiled=True)
    date_ratio = returned[0]
    peak = returned[1]
    return (date_ratio, peak)


def solution(mesh):
    placed = (P(("wide", "narrow"), None), P(("wide", "narrow"), None), P(), P(), P())
    return jax.shard_map(
        per_device,
        mesh=mesh,
        in_specs=placed,
        out_specs=(P(("wide", "narrow"), None), P(("wide", "narrow"), None)),
        check_vma=False,
    )
```

profile of v0, /device:TPU:0, one launch (start us, length us, event | category | flops | bytes accessed | tf_op | source)
XLA Modules:
  0.0 109.6 jit_solution(6393028635520491719)
XLA Ops:
  0.6 0.9 all_to_all.37
  1.5 0.2 copy.59
  1.7 0.8 reshape.2545
  2.4 7.3 %all-to-all-start = ((s32[32,1,256]{2,1,0:T(1,128)}), s32[32,1,256]{2,1,0:T(1,128)S(1)}, u32[]{:S(2)}, u32[]{:S(2)}) async-start(s32[32,1,256]{2,1,0:T(1,128)} %reshape.2545), calls=%async_computation | async-start | bytes 65536 | tf_op jit(solution)/shard_map/all_to_all | solution.py:88
  9.8 0.1 fusion.97
  11.3 2.3 %copy.58 = f32[2,32,8,512]{3,2,0,1:T(8,128)} copy(f32[2,32,8,512]{3,2,1,0:T(8,128)} %bitcast.465) | data formatting | bytes 2097152 | tf_op jit(solution)/shard_map/all_to_all | solution.py:87
  13.7 3.3 %all-to-all-done = s32[32,1,256]{2,1,0:T(1,128)S(1)} async-done(((s32[32,1,256]{2,1,0:T(1,128)}), s32[32,1,256]{2,1,0:T(1,128)S(1)}, u32[]{:S(2)}, u32[]{:S(2)}) %all-to-all-start) | async-done | bytes 32800 | tf_op jit(solution)/shard_map/all_to_all | solution.py:88
  17.0 2.6 %all-to-all-start.1 = ((f32[16,32,512]{2,0,1:T(8,128)}), f32[16,32,512]{2,0,1:T(8,128)S(1)}, u32[]{:S(2)}, u32[]{:S(2)}) async-start(f32[16,32,512]{2,0,1:T(8,128)} %bitcast.446), calls=%async_computation.1 | async-start | bytes 2097152 | tf_op jit(solution)/shard_map/all_to_all | solution.py:87
  19.9 0.5 broadcast.145
  20.5 0.7 reduce.1
  21.4 0.1 shift_right_arithmetic.35
  21.5 0.3 copy.33
  21.9 0.3 fusion.14
  22.3 1.1 %fusion.15 = f32[8,8,512]{2,1,0:T(8,128)S(1)} fusion(f32[512,512,1]{0,1,2:T(8,128)S(1)} %bitcast.457, f32[512,8]{0,1:T(8,128)S(1)} %stack.10), kind=kOutput, calls=%fused_computation.26 | convolution fusion | flops 201359360 | bytes 1196032 | tf_op jit(solution)/shard_map/dot_general | solution.py:67
  23.6 22.3 %all-to-all-done.1 = f32[16,32,512]{2,0,1:T(8,128)S(1)} async-done(((f32[16,32,512]{2,0,1:T(8,128)}), f32[16,32,512]{2,0,1:T(8,128)S(1)}, u32[]{:S(2)}, u32[]{:S(2)}) %all-to-all-start.1) | async-done | bytes 1048608 | tf_op jit(solution)/shard_map/all_to_all | solution.py:87
  45.9 0.2 bitcast_multiply_fusion
  46.1 0.6 fusion.126
  46.7 0.2 subtract_divide_fusion.6
  47.0 0.2 bitcast_divide_fusion.1
  47.2 1.3 %fusion.1 = (f32[512]{0:T(512)S(1)}, f32[512,512]{1,0:T(8,128)S(1)}) fusion(s32[512,512]{1,0:T(8,128)S(1)} %copy.33, f32[512]{0:T(512)S(1)} %fusion.100, s32[512]{0:T(512)S(1)} %shift_right_arithmetic.38, f32[512,512]{1,0:T(8,128)S(1)} %bitcast.453, f32[512,8]{0,1:T(8,128)S(1)} %stack.10, f32[8,512]{1,0:T(8,128)S(1)} %stack.11), kind=kOutput, calls=%fused_computation.4 | convolution fusion | flops 27524608 | bytes 3184640 | tf_op jit(solution)/shard_map/dot_general | solution.py:72
  48.5 1.1 fusion.9
  49.6 0.3 copy.36
  49.9 0.4 select_bitcast_fusion
  50.4 0.7 fusion.4
  51.2 0.6 copy.38
  51.9 0.2 pad_maximum_fusion
  52.1 2.4 %copy.39 = f32[2,512,512]{2,0,1:T(2,128)} copy(f32[2,512,512]{1,2,0:T(8,128)S(1)} %pad_maximum_fusion) | data formatting | bytes 4194304 | tf_op jit(solution)/shard_map/stack | solution.py:90
  54.5 52.2 %all_to_all.50 = f32[2,512,512]{2,0,1:T(2,128)S(1)} all-to-all(f32[2,512,512]{2,0,1:T(2,128)} %copy.39), channel_id=1, replica_groups=mesh['wide'=8,'narrow'=4] {'wide','narrow'}, dimensions={1} | all-to-all | bytes 4194304 | tf_op jit(solution)/shard_map/all_to_all | solution.py:91
  106.8 0.4 copy.40
  107.2 0.3 fusion.125
  107.5 1.1 copy.49
  108.5 1.0 copy.48
  (29 shorter events, 1.3 us)
Async XLA Ops:
  2.4 14.6 %all-to-all-start = ((s32[32,1,256]{2,1,0:T(1,128)}), s32[32,1,256]{2,1,0:T(1,128)S(1)}, u32[]{:S(2)}, u32[]{:S(2)}) async-start(s32[32,1,256]{2,1,0:T(1,128)} %reshape.2545), calls=%async_computation | async-start | bytes 65536 | tf_op jit(solution)/shard_map/all_to_all | solution.py:88
  11.3 8.6 %copy-start = (s32[512]{0:T(512)S(1)}, s32[512]{0:T(512)}, u32[]{:S(2)}) copy-start(s32[512]{0:T(512)} %param.9) | copy-start | bytes 6148
  17.0 28.8 %all-to-all-start.1 = ((f32[16,32,512]{2,0,1:T(8,128)}), f32[16,32,512]{2,0,1:T(8,128)S(1)}, u32[]{:S(2)}, u32[]{:S(2)}) async-start(f32[16,32,512]{2,0,1:T(8,128)} %bitcast.446), calls=%async_computation.1 | async-start | bytes 2097152 | tf_op jit(solution)/shard_map/all_to_all | solution.py:87
where the time goes:
time: 110 us
  blocking collectives  52.2 us (47%)
  waiting for transfers between devices  25.6 us (23%)
  local copies, waits for them, and re-layouts  11.9 us (11%)
  starting transfers between devices  9.97 us (9%)
  matrix products  4.08 us (4%)
  other arithmetic  3.62 us (3%)
  between operations  2.2 us (2%)
    all_to_all x1, blocking collectives, per_device(): lax.all_to_all(outgoing, ('wide', 'narrow'), split_axis=1, concat_axis=2,...  52.2 us
    all_to_all x1, waiting for transfers between devices, per_device(): lax.all_to_all(values, ('wide', 'narrow'), split_axis=1, concat_axis=0, t...  22.3 us
    all_to_all x1, starting transfers between devices, per_device(): lax.all_to_all(cloud_words, ('wide', 'narrow'), split_axis=1, concat_axis...  7.33 us
    all_to_all x1, waiting for transfers between devices, per_device(): lax.all_to_all(cloud_words, ('wide', 'narrow'), split_axis=1, concat_axis...  3.31 us
    unnamed x8, local copies, waits for them, and re-layouts  3.07 us
    another operation x2, local copies, waits for them, and re-layouts, per_device(): outgoing = jnp.stack([ratio, lax.cummax(jnp.abs(ratio), axis=0)])  3.02 us
    all_to_all x1, starting transfers between devices, per_device(): lax.all_to_all(values, ('wide', 'narrow'), split_axis=1, concat_axis=0, t...  2.65 us
    all_to_all x1, local copies, waits for them, and re-layouts, per_device(): lax.all_to_all(values, ('wide', 'narrow'), split_axis=1, concat_axis=0, t...  2.3 us
  transfers between devices with their start and end apart: 2, of which 2 were waited for; matrix products, arithmetic and copies ran while one was open for 6% of the time, Pallas kernels for 0%

commit v1 on v0

v1 whole, which is shorter than its diff:
```python
import functools
import math

import jax
import jax.numpy as jnp
import numpy as np
from jax import lax
from jax.experimental import pallas as pl
from jax.experimental.pallas import tpu as pltpu
from jax.sharding import PartitionSpec as P

PERIOD = 46
HARMONICS = 3
COLS = 8
WINDOW = 64
WORD = 32
AXES = ("wide", "narrow")
HIGH = lax.Precision.HIGHEST


def design_table(dates):
    day = np.arange(dates).astype(np.float32)
    columns = [np.ones((dates,), np.float32), day / np.float32(dates)]
    for harmonic in range(1, HARMONICS + 1):
        phases = (np.float32(2.0 * math.pi * harmonic / PERIOD) * day).astype(np.float64)
        columns.append(np.cos(phases).astype(np.float32))
        columns.append(np.sin(phases).astype(np.float32))
    return np.stack(columns, axis=1)


def outer_table(design):
    rows = [design[:, i] * design[:, j] for i in range(COLS) for j in range(i + 1)]
    while len(rows) % 8:
        rows.append(np.zeros_like(rows[0]))
    return np.stack(rows, axis=0)


def spread_table(pixels):
    words = pixels // WORD
    pixel = np.arange(pixels)
    table = np.zeros((4, words, pixels), np.float32)
    table[(pixel % WORD) // 8, pixel // WORD, pixel] = 1.0
    return table.reshape(4 * words, pixels)


def unpack_clear(words, spread):
    planes = [jnp.bitwise_and(jnp.right_shift(words, 8 * k), 255).astype(jnp.float32) for k in range(4)]
    byte_of = jnp.dot(jnp.concatenate(planes, axis=1).astype(jnp.bfloat16), spread, preferred_element_type=jnp.float32)
    bit = jnp.bitwise_and(lax.broadcasted_iota(jnp.int32, byte_of.shape, 1), 7)
    return jnp.bitwise_and(jnp.right_shift(byte_of.astype(jnp.int32), bit), 1).astype(jnp.float32)


def solve_rows(normal, target):
    factor = {}
    inverse = []
    for col in range(COLS):
        for row in range(col, COLS):
            summed = normal(row, col)
            for mid in range(col):
                summed = summed - factor[row, mid] * factor[col, mid]
            if row == col:
                inverse.append(1.0 / jnp.sqrt(summed))
            else:
                factor[row, col] = summed * inverse[col]
    forward = []
    for row in range(COLS):
        summed = target(row)
        for mid in range(row):
            summed = summed - factor[row, mid] * forward[mid]
        forward.append(summed * inverse[row])
    solved = [None] * COLS
    for row in reversed(range(COLS)):
        summed = forward[row]
        for mid in range(row + 1, COLS):
            summed = summed - factor[mid, row] * solved[mid]
        solved[row] = summed * inverse[row]
    return solved


def fit_kernel(history_ref, values_ref, words_ref, spread_ref, outer_ref, turned_ref, design_ref, stats_ref):
    clear = unpack_clear(words_ref[...], spread_ref[...])
    day = lax.broadcasted_iota(jnp.int32, clear.shape, 0)
    weight = jnp.where(day < history_ref[0], clear, 0.0)
    values = values_ref[...]
    normal = jnp.dot(outer_ref[...], weight, precision=HIGH, preferred_element_type=jnp.float32)
    target = jnp.dot(turned_ref[...], weight * values, precision=HIGH, preferred_element_type=jnp.float32)
    solved = solve_rows(
        lambda i, j: normal[i * (i + 1) // 2 + j][None, :],
        lambda i: target[i][None, :],
    )
    for i in range(COLS):
        stats_ref[i : i + 1, :] = solved[i]
    coeffs = stats_ref[0:COLS, :]
    fitted = jnp.dot(design_ref[...], coeffs, precision=HIGH, preferred_element_type=jnp.float32)
    resid = weight * (values - fitted)
    squares = jnp.sum(resid * resid, axis=0, keepdims=True)
    count = normal[0:1, :]
    sigma = jnp.sqrt(squares / (count - COLS) + 1e-06)
    stats_ref[COLS : COLS + 1, :] = 1.0 / (sigma * jnp.sqrt(count))
    stats_ref[COLS + 1 :, :] = jnp.zeros_like(stats_ref[COLS + 1 :, :])


def ratio_kernel(values_ref, words_ref, early_ref, early_words_ref, stats_ref, spread_ref, design_ref, late_ref, ratio_ref, carry_ref):
    spread = spread_ref[...]
    fitted = jnp.dot(design_ref[...], stats_ref[0:COLS, :], precision=HIGH, preferred_element_type=jnp.float32)
    before = unpack_clear(early_words_ref[...], spread) * (early_ref[...] - fitted[:WINDOW])
    after = unpack_clear(words_ref[...], spread) * (values_ref[...] - fitted[WINDOW:])
    moving = jnp.concatenate([before, after], axis=0)
    span = 1
    while span < WINDOW:
        moving = moving + pltpu.roll(moving, span, 0)
        span *= 2
    ratio = moving[WINDOW:] * stats_ref[COLS : COLS + 1, :] * late_ref[:, 0:1]
    ratio_ref[...] = ratio
    blocks = carry_ref.shape[0]
    per_block = ratio.shape[0] // blocks
    running = jnp.zeros((1, ratio.shape[1]), jnp.float32)
    for block in range(blocks):
        carry_ref[block : block + 1, :] = running
        top = jnp.max(jnp.abs(ratio[block * per_block : (block + 1) * per_block]), axis=0, keepdims=True)
        running = jnp.maximum(running, top)


def finish_kernel(upper_ref, ratio_ref, carry_ref, out_ref, peak_ref):
    blocks, rows, width = ratio_ref.shape
    upper = upper_ref[0] > 0
    for block in range(blocks):
        at = slice(block * width, (block + 1) * width)
        ratio = jnp.where(upper, ratio_ref[block], 0.0)
        peak = jnp.maximum(jnp.abs(ratio), jnp.where(upper, carry_ref[block : block + 1, :], 0.0))
        row = lax.broadcasted_iota(jnp.int32, peak.shape, 0)
        span = 1
        while span < rows:
            peak = jnp.maximum(peak, jnp.where(row >= span, pltpu.roll(peak, span, 0), 0.0))
            span *= 2
        out_ref[:, at] = ratio
        peak_ref[:, at] = peak


SMEM = pl.BlockSpec(memory_space=pltpu.SMEM)
VMEM = pl.BlockSpec(memory_space=pltpu.VMEM)


def f32(*shape):
    return jax.ShapeDtypeStruct(shape, jnp.float32)


def per_device(values, cloud_words, history_len, monitor_start, boundary_table, devices):
    rows, pixels = values.shape
    dates = boundary_table.shape[0]
    half = devices // 2
    late = dates // 2
    width = pixels // half
    words = width // WORD
    groups = [list(range(half)), list(range(half, devices))]
    upward = [(i, i + half) for i in range(half)]
    design = design_table(dates)
    spread = jnp.asarray(spread_table(width), jnp.bfloat16)

    def exchange(blocks):
        return lax.all_to_all(blocks, AXES, 0, 0, axis_index_groups=groups, tiled=True)

    sent_words = cloud_words.reshape(rows, half, words).transpose(1, 0, 2).reshape(half, rows * words)
    own_words = exchange(sent_words).reshape(late, words)
    own = exchange(values.reshape(rows, half, width).transpose(1, 0, 2)).reshape(late, width)
    early = lax.ppermute(own[late - WINDOW :], AXES, upward)
    early_words = lax.ppermute(own_words[late - WINDOW :], AXES, upward)
    stats = pl.pallas_call(
        fit_kernel,
        out_shape=f32(2 * COLS, width),
        in_specs=[SMEM] + [VMEM] * 6,
        out_specs=VMEM,
        name="fit",
    )(history_len, own, own_words, spread, outer_table(design[:late]), design[:late].T, design[:late])
    stats = lax.ppermute(stats, AXES, upward)
    day = jnp.arange(late, dtype=jnp.int32) + late
    factor = jnp.where(day >= monitor_start[0], 1.0 / (boundary_table[late:].astype(jnp.float32) * 0.001), 0.0)
    factor = jnp.broadcast_to(factor[:, None], (late, 128))
    ratio, carry = pl.pallas_call(
        ratio_kernel,
        out_shape=(f32(late, width), f32(half, width)),
        in_specs=[VMEM] * 8,
        out_specs=(VMEM, VMEM),
        name="ratio",
    )(own, own_words, early, early_words, stats, spread, design[late - WINDOW :], factor)
    ratio = exchange(ratio.reshape(half, rows, width))
    carry = exchange(carry)
    upper = (lax.axis_index(AXES) >= half).astype(jnp.int32).reshape(1)
    return pl.pallas_call(
        finish_kernel,
        out_shape=(f32(rows, pixels), f32(rows, pixels)),
        in_specs=[SMEM, VMEM, VMEM],
        out_specs=(VMEM, VMEM),
        name="finish",
    )(upper, ratio, carry)


def solution(mesh):
    placed = (P(AXES, None), P(AXES, None), P(), P(), P())
    return jax.shard_map(
        functools.partial(per_device, devices=mesh.size),
        mesh=mesh,
        in_specs=placed,
        out_specs=(P(AXES, None), P(AXES, None)),
        check_vma=False,
    )
```

time: 110 us -> 92.2 us (0.84)
  blocking collectives: 52.2 us -> 12.6 us
  starting transfers between devices: 9.97 us -> 23.6 us
  Pallas kernels: 0 us -> 13 us
  waiting for transfers between devices: 25.6 us -> 32.9 us
  local copies, waits for them, and re-layouts: 11.9 us -> 7.33 us
  matrix products: 4.08 us -> 0 us
  other arithmetic: 3.62 us -> 0.08 us
    all_to_all x1, blocking collectives: 52.2 us -> 12.6 us  [exchange(): lax.all_to_all(blocks, AXES, 0, 0, axis_index_groups=groups, tiled=True)]
    pallas_call x0 -> x3, Pallas kernels: none -> 13 us  [the longest x1 5.12 us: per_device(): pl.pallas_call(fit_kernel, out_shape=f32(2 * COLS, width), in_specs=[SMEM...]
    ppermute x0 -> x3, starting transfers between devices: none -> 10 us  [the longest x1 4.51 us: per_device(): early = lax.ppermute(own[late - WINDOW:], AXES, upward)]
    all_to_all x2 -> x3, waiting for transfers between devices: 25.6 us -> 30.7 us  [exchange(): lax.all_to_all(blocks, AXES, 0, 0, axis_index_groups=groups, tiled=True)]
    dot_general x4 -> x0, matrix products: 4.08 us -> none  [the longest x1 1.28 us: fit_statistic(): jnp.dot(design, coeffs, precision=HIGH, preferred_element_type=jnp.float32)]
    all_to_all x2 -> x3, starting transfers between devices: 9.97 us -> 13.6 us  [exchange(): lax.all_to_all(blocks, AXES, 0, 0, axis_index_groups=groups, tiled=True)]
    reshape x0 -> x4, local copies, waits for them, and re-layouts: none -> 3.18 us  [the longest x1 2.31 us: per_device(): values.reshape(rows, half, width).transpose(1, 0, 2)]
    another operation x7 -> x0, local copies, waits for them, and re-layouts: 3.11 us -> none  [the longest x2 3.02 us: per_device(): outgoing = jnp.stack([ratio, lax.cummax(jnp.abs(ratio), axis=0)])]
  transfers between devices with their start and end apart: 2 -> 6, of which waited for: 2 -> 3; matrix products, arithmetic and copies ran while one was open for 6% -> 2% of each run, Pallas kernels for 0% -> 6%
where the time goes in v1:
time: 92.2 us; the launch traced here: 91.5 us
  waiting for transfers between devices  32.9 us (36%)
  starting transfers between devices  23.6 us (26%)
  Pallas kernels  13 us (14%)
  blocking collectives  12.6 us (14%)
  local copies, waits for them, and re-layouts  7.33 us (8%)
  between operations  2.07 us (2%)
    all_to_all x3, waiting for transfers between devices, exchange(): lax.all_to_all(blocks, AXES, 0, 0, axis_index_groups=groups, tiled=True)  30.7 us
    all_to_all x3, starting transfers between devices, exchange(): lax.all_to_all(blocks, AXES, 0, 0, axis_index_groups=groups, tiled=True)  13.6 us
    all_to_all x1, blocking collectives, exchange(): lax.all_to_all(blocks, AXES, 0, 0, axis_index_groups=groups, tiled=True)  12.6 us
    pallas_call x1, Pallas kernels, per_device(): pl.pallas_call(fit_kernel, out_shape=f32(2 * COLS, width), in_specs=[SMEM...  5.12 us
    pallas_call x1, Pallas kernels, per_device(): pl.pallas_call(ratio_kernel, out_shape=(f32(late, width), f32(half, width...  4.89 us
    ppermute x1, starting transfers between devices, per_device(): early = lax.ppermute(own[late - WINDOW:], AXES, upward)  4.51 us
    ppermute x1, starting transfers between devices, per_device(): early_words = lax.ppermute(own_words[late - WINDOW:], AXES, upward)  4.24 us
    pallas_call x1, Pallas kernels, per_device(): pl.pallas_call(finish_kernel, out_shape=(f32(rows, pixels), f32(rows, pix...  2.95 us
  transfers between devices with their start and end apart: 6, of which 3 were waited for; matrix products, arithmetic and copies ran while one was open for 2% of the time, Pallas kernels for 6%

profile of v1, /device:TPU:0, one launch (start us, length us, event | category | flops | bytes accessed | tf_op | source)
XLA Modules:
  0.0 91.5 jit_solution(16378859261549534041)
XLA Ops:
  0.6 2.3 %copy.24 = f32[2,16,8,1024]{3,2,0,1:T(8,128)} copy(f32[2,16,8,1024]{3,2,1,0:T(8,128)} %bitcast.22) | data formatting | bytes 2097152 | tf_op jit(solution)/shard_map/reshape | solution.py:165
  2.9 6.4 %all-to-all-start = ((f32[16,16,1024]{2,1,0:T(8,128)}), f32[16,16,1024]{2,1,0:T(8,128)S(1)}, u32[]{:S(2)}, u32[]{:S(2)}) async-start(f32[16,16,1024]{2,1,0:T(8,128)} %bitcast.16), calls=%async_computation | async-start | bytes 2097152 | tf_op jit(solution)/shard_map/all_to_all | solution.py:161
  9.4 0.0 copy-done.5
  9.4 0.1 reshape.40
  9.6 0.7 all_to_all.20
  10.3 15.2 %all-to-all-done = f32[16,16,1024]{2,1,0:T(8,128)S(1)} async-done(((f32[16,16,1024]{2,1,0:T(8,128)}), f32[16,16,1024]{2,1,0:T(8,128)S(1)}, u32[]{:S(2)}, u32[]{:S(2)}) %all-to-all-start) | async-done | bytes 1048608 | tf_op jit(solution)/shard_map/all_to_all | solution.py:161
  25.5 3.5 %all-to-all-start.1 = ((s32[16,1,512]{2,1,0:T(1,128)}), s32[16,1,512]{2,1,0:T(1,128)S(1)}, u32[]{:S(2)}, u32[]{:S(2)}) async-start(s32[16,1,512]{2,1,0:T(1,128)} %all_to_all.20), calls=%async_computation.1 | async-start | bytes 65536 | tf_op jit(solution)/shard_map/all_to_all | solution.py:161
  30.4 4.5 %collective-permute-start = (f32[64,1024]{1,0:T(8,128)S(1)}, f32[64,1024]{1,0:T(8,128)S(1)}, u32[]{:S(2)}, u32[]{:S(2)}) collective-permute-start(f32[64,1024]{1,0:T(8,128)S(1)} %bitcast.26), channel_id=1, source_target_pairs={{0,16},{1,17},{2,18},{3,19},{4,20},{5,21},{6,22},{7,23},{8,24},{9,... | collective-permute-start | bytes 786440 | tf_op jit(solution)/shard_map/ppermute | solution.py:166
  34.9 0.0 all-to-all-done.1
  34.9 0.1 slice.19
  35.0 4.2 %collective-permute-start.1 = (s32[64,32]{1,0:T(8,128)S(1)}, s32[64,32]{1,0:T(8,128)S(1)}, u32[]{:S(2)}, u32[]{:S(2)}) collective-permute-start(s32[64,32]{1,0:T(8,128)S(1)} %slice.19), channel_id=1, source_target_pairs={{0,16},{1,17},{2,18},{3,19},{4,20},{5,21},{6,22},{7,23},{8,24},{9,... | collective-permute-start | bytes 24584 | tf_op jit(solution)/shard_map/ppermute | solution.py:167
  39.2 0.1 reduce
  39.3 0.7 reshape.41.words_ref
  40.1 0.0 copy-done
  40.1 5.1 %fit.1 = f32[16,1024]{1,0:T(8,128)} custom-call(s32[1]{0:T(128)S(6)} %copy.27.history_ref, f32[256,1024]{1,0:T(8,128)} %bitcast.20, s32[256,32]{1,0:T(8,128)} %reshape.41.words_ref, bf16[128,1024]{1,0:T(8,128)(2,1)} %constant.31.clone.spread_ref, f32[40,256]{1,0:T(8,128)} %constant.32.clone.outer_ref, f32[8,256]{1,0:T(8,128)} %constant.33.clone.turned_ref, ...), custom_call_target="tpu_custom_call" | custom-call | tf_op jit(solution)/shard_map/fit/pallas_call | solution.py:168
  45.2 1.3 %collective-permute-start.2 = (f32[16,1024]{1,0:T(8,128)}, f32[16,1024]{1,0:T(8,128)S(1)}, u32[]{:S(2)}, u32[]{:S(2)}) collective-permute-start(f32[16,1024]{1,0:T(8,128)} %fit.1), channel_id=1, source_target_pairs={{0,16},{1,17},{2,18},{3,19},{4,20},{5,21},{6,22},{7,23},{8,24},{9,... | collective-permute-start | bytes 196616 | tf_op jit(solution)/shard_map/ppermute | solution.py:175
  46.5 0.0 copy-done.6
  46.5 0.0 collective-permute-done.1.early_words_ref
  46.5 0.0 copy-start.4
  46.5 2.2 %collective-permute-done.2.stats_ref = f32[16,1024]{1,0:T(8,128)S(1)} collective-permute-done((f32[16,1024]{1,0:T(8,128)}, f32[16,1024]{1,0:T(8,128)S(1)}, u32[]{:S(2)}, u32[]{:S(2)}) %collective-permute-start.2) | collective-permute-done | bytes 65568 | tf_op jit(solution)/shard_map/ppermute | solution.py:175
  48.7 0.0 collective-permute-done.early_ref
  48.7 0.8 broadcast_in_dim.11.late_ref
  49.5 0.0 copy-done.4
  49.5 0.0 copy-done.3
  49.5 4.9 %ratio.1 = (f32[256,1024]{1,0:T(8,128)}, f32[16,1024]{1,0:T(8,128)}) custom-call(f32[256,1024]{1,0:T(8,128)} %bitcast.21, s32[256,32]{1,0:T(8,128)} %reshape.41.words_ref, f32[64,1024]{1,0:T(8,128)} %copy-done.2, s32[64,32]{1,0:T(8,128)} %copy-done.4, f32[16,1024]{1,0:T(8,128)} %copy-done.3, bf16[128,1024]{1,0:T(8,128)(2,1)} %constant.31.clone.spread_ref, ...), custom_call_target="tpu_custom_call" | custom-call | tf_op jit(solution)/shard_map/ratio/pallas_call | solution.py:179
  54.4 0.9 copy.18
  55.3 12.6 %all_to_all.30 = f32[16,1,1024]{2,1,0:T(1,128)S(1)} all-to-all(f32[16,1,1024]{2,1,0:T(1,128)S(1)} %copy.18), channel_id=1, replica_groups={{0,1,2,3,4,5,6,7,8,9,10,11,12,13,14,15},{16,17,18,19,20,21,22,23,24,25,..., dimensions={0} | all-to-all | bytes 131072 | tf_op jit(solution)/shard_map/all_to_all | solution.py:161
  67.8 3.7 %all-to-all-start.2 = ((f32[16,16,1024]{2,1,0:T(8,128)}), f32[16,16,1024]{2,1,0:T(8,128)S(1)}, u32[]{:S(2)}, u32[]{:S(2)}) async-start(f32[16,16,1024]{2,1,0:T(8,128)} %bitcast.23), calls=%async_computation.2 | async-start | bytes 2097152 | tf_op jit(solution)/shard_map/all_to_all | solution.py:161
  71.5 0.6 copy.26
  72.1 15.5 %all-to-all-done.2.ratio_ref = f32[16,16,1024]{2,1,0:T(8,128)S(1)} async-done(((f32[16,16,1024]{2,1,0:T(8,128)}), f32[16,16,1024]{2,1,0:T(8,128)S(1)}, u32[]{:S(2)}, u32[]{:S(2)}) %all-to-all-start.2) | async-done | bytes 1048608 | tf_op jit(solution)/shard_map/all_to_all | solution.py:161
  87.6 1.0 %copy-done.1 = f32[16,16,1024]{2,1,0:T(8,128)} copy-done((f32[16,16,1024]{2,1,0:T(8,128)}, f32[16,16,1024]{2,1,0:T(8,128)S(1)}, u32[]{:S(2)}) %copy-start.1) | copy-done | bytes 1048600
  88.6 2.9 %finish.1 = (f32[16,16384]{1,0:T(8,128)}, f32[16,16384]{1,0:T(8,128)}) custom-call(s32[1]{0:T(128)} %bitcast.upper_ref, f32[16,16,1024]{2,1,0:T(8,128)} %copy-done.1, f32[16,1024]{1,0:T(8,128)} %bitcast.25), custom_call_target="tpu_custom_call" | custom-call | tf_op jit(solution)/shard_map/finish/pallas_call | solution.py:189
  (11 shorter events, 0.1 us)
Async XLA Ops:
  2.9 6.5 %copy-start.5 = (s32[16,512]{1,0:T(8,128)S(1)}, s32[16,512]{1,0:T(8,128)}, u32[]{:S(2)}) copy-start(s32[16,512]{1,0:T(8,128)} %param.11) | copy-start | bytes 98308
  2.9 22.6 %all-to-all-start = ((f32[16,16,1024]{2,1,0:T(8,128)}), f32[16,16,1024]{2,1,0:T(8,128)S(1)}, u32[]{:S(2)}, u32[]{:S(2)}) async-start(f32[16,16,1024]{2,1,0:T(8,128)} %bitcast.16), calls=%async_computation | async-start | bytes 2097152 | tf_op jit(solution)/shard_map/all_to_all | solution.py:161
  25.5 14.5 %copy-start = (f32[16,16,1024]{2,1,0:T(8,128)}, f32[16,16,1024]{2,1,0:T(8,128)S(1)}, u32[]{:S(2)}) copy-start(f32[16,16,1024]{2,1,0:T(8,128)S(1)} %all-to-all-done) | copy-start | bytes 3145732
  25.5 9.3 %all-to-all-start.1 = ((s32[16,1,512]{2,1,0:T(1,128)}), s32[16,1,512]{2,1,0:T(1,128)S(1)}, u32[]{:S(2)}, u32[]{:S(2)}) async-start(s32[16,1,512]{2,1,0:T(1,128)} %all_to_all.20), calls=%async_computation.1 | async-start | bytes 65536 | tf_op jit(solution)/shard_map/all_to_all | solution.py:161
  30.4 18.3 %collective-permute-start = (f32[64,1024]{1,0:T(8,128)S(1)}, f32[64,1024]{1,0:T(8,128)S(1)}, u32[]{:S(2)}, u32[]{:S(2)}) collective-permute-start(f32[64,1024]{1,0:T(8,128)S(1)} %bitcast.26), channel_id=1, source_target_pairs={{0,16},{1,17},{2,18},{3,19},{4,20},{5,21},{6,22},{7,23},{8,24},{9,... | collective-permute-start | bytes 786440 | tf_op jit(solution)/shard_map/ppermute | solution.py:166
  35.0 11.5 %collective-permute-start.1 = (s32[64,32]{1,0:T(8,128)S(1)}, s32[64,32]{1,0:T(8,128)S(1)}, u32[]{:S(2)}, u32[]{:S(2)}) collective-permute-start(s32[64,32]{1,0:T(8,128)S(1)} %slice.19), channel_id=1, source_target_pairs={{0,16},{1,17},{2,18},{3,19},{4,20},{5,21},{6,22},{7,23},{8,24},{9,... | collective-permute-start | bytes 24584 | tf_op jit(solution)/shard_map/ppermute | solution.py:167
  40.1 6.4 %copy-start.6 = (s32[512]{0:T(512)S(1)}, s32[512]{0:T(512)}, u32[]{:S(2)}) copy-start(s32[512]{0:T(512)} %param.14) | copy-start | bytes 6148
  45.2 3.5 %collective-permute-start.2 = (f32[16,1024]{1,0:T(8,128)}, f32[16,1024]{1,0:T(8,128)S(1)}, u32[]{:S(2)}, u32[]{:S(2)}) collective-permute-start(f32[16,1024]{1,0:T(8,128)} %fit.1), channel_id=1, source_target_pairs={{0,16},{1,17},{2,18},{3,19},{4,20},{5,21},{6,22},{7,23},{8,24},{9,... | collective-permute-start | bytes 196616 | tf_op jit(solution)/shard_map/ppermute | solution.py:175
  46.5 2.9 %copy-start.4 = (s32[64,32]{1,0:T(8,128)}, s32[64,32]{1,0:T(8,128)S(1)}, u32[]{:S(2)}) copy-start(s32[64,32]{1,0:T(8,128)S(1)} %collective-permute-done.1.early_words_ref) | copy-start | bytes 24580
  48.7 0.8 copy-start.3
  48.7 0.8 copy-start.2
  67.8 19.8 %all-to-all-start.2 = ((f32[16,16,1024]{2,1,0:T(8,128)}), f32[16,16,1024]{2,1,0:T(8,128)S(1)}, u32[]{:S(2)}, u32[]{:S(2)}) async-start(f32[16,16,1024]{2,1,0:T(8,128)} %bitcast.23), calls=%async_computation.2 | async-start | bytes 2097152 | tf_op jit(solution)/shard_map/all_to_all | solution.py:161
  87.6 1.0 %copy-start.1 = (f32[16,16,1024]{2,1,0:T(8,128)}, f32[16,16,1024]{2,1,0:T(8,128)S(1)}, u32[]{:S(2)}) copy-start(f32[16,16,1024]{2,1,0:T(8,128)S(1)} %all-to-all-done.2.ratio_ref) | copy-start | bytes 3145732

commit v2 on v1

v2 whole, which is shorter than its diff:
```python
import functools
import math

import jax
import jax.numpy as jnp
import ml_dtypes
import numpy as np
from jax import lax
from jax.experimental import pallas as pl
from jax.experimental.pallas import tpu as pltpu
from jax.sharding import PartitionSpec as P

PERIOD = 46
HARMONICS = 3
COLS = 8
WINDOW = 64
WORD = 32
LANES = 128
SUB = 8
STEPS = 4
AXES = ("wide", "narrow")


def design_table(dates):
    day = np.arange(dates).astype(np.float32)
    columns = [np.ones((dates,), np.float32), day / np.float32(dates)]
    for harmonic in range(1, HARMONICS + 1):
        phases = (np.float32(2.0 * math.pi * harmonic / PERIOD) * day).astype(np.float64)
        columns.append(np.cos(phases).astype(np.float32))
        columns.append(np.sin(phases).astype(np.float32))
    return np.stack(columns, axis=1)


def outer_table(design):
    rows = [design[:, i] * design[:, j] for i in range(COLS) for j in range(i + 1)]
    while len(rows) % SUB:
        rows.append(np.zeros_like(rows[0]))
    return np.stack(rows, axis=0)


def split_table(table):
    parts = []
    rest = table
    for _ in range(3):
        part = rest.astype(ml_dtypes.bfloat16)
        parts.append(part)
        rest = rest - part.astype(np.float32)
    return parts


def split_rows(array):
    high = array.astype(jnp.bfloat16).astype(jnp.float32)
    rest = array - high
    mid = rest.astype(jnp.bfloat16).astype(jnp.float32)
    return high, mid, rest - mid


def spread_table(pixels, slots):
    pixel = np.arange(pixels)
    byte = (pixel % WORD) // 8
    table = np.zeros((slots, 2 * LANES, pixels), np.float32)
    for slot in range(slots):
        table[slot, (byte % 2) * LANES + 64 * slot + 32 * (byte // 2) + pixel // WORD, pixel] = 1.0
    return table.astype(ml_dtypes.bfloat16)


def flat_rows(blocks):
    count, rows, lanes = blocks.shape
    if rows % SUB == 0:
        return blocks.reshape(count * rows, lanes)
    return jnp.concatenate([blocks[i] for i in range(count)], axis=0)


def read_values(message, rows):
    tiles = (message.shape[1] - SUB) // rows
    return jnp.concatenate([flat_rows(message[:, c * rows : (c + 1) * rows]) for c in range(tiles)], axis=1)


def read_clear(message, rows, spread_ref):
    blocks = message.shape[0]
    halves = message[:, -SUB:].reshape(blocks * SUB, LANES).astype(jnp.int32)
    planes = [jnp.bitwise_and(halves, 255), jnp.right_shift(halves, 8)]
    planes = jnp.concatenate([plane.astype(jnp.float32) for plane in planes], axis=1).astype(jnp.bfloat16)
    found = []
    for slot in range(spread_ref.shape[0]):
        byte = jnp.dot(planes, spread_ref[slot], preferred_element_type=jnp.float32).astype(jnp.int32)
        bit = jnp.bitwise_and(lax.broadcasted_iota(jnp.int32, byte.shape, 1), 7)
        flags = jnp.bitwise_and(jnp.right_shift(byte, bit), 1).astype(jnp.float32)
        found.append(flags.reshape(blocks, SUB, -1)[:, : min(rows, SUB)])
    return flat_rows(jnp.concatenate(found, axis=1))


def fit_dot(design_ref, coeffs):
    high, mid, low = split_rows(coeffs)
    stacked = jnp.concatenate([high, high, high, mid, mid, low], axis=0).astype(jnp.bfloat16)
    return jnp.dot(design_ref[...], stacked, preferred_element_type=jnp.float32)


def six_wide(design):
    high, mid, low = split_table(design)
    return np.concatenate([high, mid, low, high, mid, high], axis=1)


def solve_rows(normal, target):
    factor = {}
    inverse = []
    for col in range(COLS):
        for row in range(col, COLS):
            summed = normal(row, col)
            for mid in range(col):
                summed = summed - factor[row, mid] * factor[col, mid]
            if row == col:
                inverse.append(1.0 / jnp.sqrt(summed))
            else:
                factor[row, col] = summed * inverse[col]
    forward = []
    for row in range(COLS):
        summed = target(row)
        for mid in range(row):
            summed = summed - factor[row, mid] * forward[mid]
        forward.append(summed * inverse[row])
    solved = [None] * COLS
    for row in reversed(range(COLS)):
        summed = forward[row]
        for mid in range(row + 1, COLS):
            summed = summed - factor[mid, row] * solved[mid]
        solved[row] = summed * inverse[row]
    return solved


def pack_kernel(values_ref, words_ref, message_ref):
    rows = values_ref.shape[0]
    blocks, length, _ = message_ref.shape
    tiles = (length - SUB) // rows
    for block in range(blocks):
        for c in range(tiles):
            start = (block * tiles + c) * LANES
            message_ref[block, c * rows : (c + 1) * rows, :] = values_ref[:, start : start + LANES]
        per_tile = LANES // WORD
        words = words_ref[:, block // per_tile * LANES : (block // per_tile + 1) * LANES]
        if rows % SUB:
            words = jnp.concatenate([words, jnp.zeros((SUB - rows % SUB, LANES), jnp.int32)], axis=0)
        quarter = lax.broadcasted_iota(jnp.int32, (SUB, LANES), 1) // WORD
        riding = jnp.zeros((SUB, LANES), jnp.int32)
        for slot in range(words.shape[0] // SUB):
            part = words[slot * SUB : (slot + 1) * SUB]
            for side in range(2):
                place = 2 * slot + side
                half = jnp.bitwise_and(jnp.right_shift(part, 16 * side), 65535)
                shift = (place - block % per_tile) * WORD % LANES
                moved = pltpu.roll(half, shift, 1) if shift else half
                riding = jnp.where(quarter == place, moved, riding)
        message_ref[block, tiles * rows :, :] = riding.astype(jnp.float32)


def fit_kernel(history_ref, message_ref, spread_ref, outer_ref, turned_ref, design_ref, stats_ref, *, rows):
    message = message_ref[...]
    clear = read_clear(message, rows, spread_ref)
    values = read_values(message, rows)
    day = lax.broadcasted_iota(jnp.int32, clear.shape, 0)
    weight = jnp.where(day < history_ref[0], clear, 0.0)
    tripled = jnp.dot(outer_ref[...], weight.astype(jnp.bfloat16), preferred_element_type=jnp.float32)
    size = tripled.shape[0] // 3
    normal = tripled[2 * size :] + tripled[size : 2 * size] + tripled[:size]
    seen = [part.astype(jnp.bfloat16) for part in split_rows(weight * values)]
    high, mid, low = [jnp.dot(turned_ref[...], part, preferred_element_type=jnp.float32) for part in seen]
    target = low[:COLS] + mid[COLS : 2 * COLS] + high[2 * COLS :]
    target = target + mid[:COLS] + high[COLS : 2 * COLS]
    target = target + high[:COLS]
    solved = solve_rows(
        lambda i, j: normal[i * (i + 1) // 2 + j][None, :],
        lambda i: target[i][None, :],
    )
    for i in range(COLS):
        stats_ref[i : i + 1, :] = solved[i]
    resid = weight * (values - fit_dot(design_ref, stats_ref[0:COLS, :]))
    squares = jnp.sum(resid * resid, axis=0, keepdims=True)
    count = normal[0:1, :]
    sigma = jnp.sqrt(squares / (count - COLS) + 1e-06)
    stats_ref[COLS : COLS + 1, :] = 1.0 / (sigma * jnp.sqrt(count))
    stats_ref[COLS + 1 :, :] = jnp.zeros_like(stats_ref[COLS + 1 :, :])


def ratio_kernel(start_ref, message_ref, early_ref, stats_ref, spread_ref, design_ref, bounds_ref, out_ref, *, rows):
    message = jnp.concatenate([early_ref[...], message_ref[...]], axis=0)
    clear = read_clear(message, rows, spread_ref)
    values = read_values(message, rows)
    moving = clear * (values - fit_dot(design_ref, stats_ref[0:COLS, :]))
    span = 1
    while span < WINDOW:
        moving = moving + pltpu.roll(moving, span, 0)
        span *= 2
    late = moving.shape[0] - WINDOW
    day = late + lax.broadcasted_iota(jnp.int32, (SUB, late), 1)
    bounds = jnp.broadcast_to(bounds_ref[:, late:].astype(jnp.float32), (SUB, late)) * 0.001
    factor = jnp.transpose(jnp.where(day >= start_ref[0], 1.0 / bounds, 0.0))[:, 0:1]
    ratio = moving[WINDOW:] * stats_ref[COLS : COLS + 1, :] * factor
    blocks = out_ref.shape[0]
    tiles = ratio.shape[1] // LANES
    running = jnp.zeros((1, ratio.shape[1]), jnp.float32)
    for block in range(blocks):
        part = ratio[block * rows : (block + 1) * rows]
        for c in range(tiles):
            at = slice(c * LANES, (c + 1) * LANES)
            out_ref[block, c * rows : (c + 1) * rows, :] = part[:, at]
            out_ref[block, tiles * rows + c : tiles * rows + c + 1, :] = running[:, at]
        running = jnp.maximum(running, jnp.max(jnp.abs(part), axis=0, keepdims=True))


def finish_kernel(upper_ref, message_ref, out_ref, peak_ref):
    blocks, length, _ = message_ref.shape
    rows = out_ref.shape[0]
    tiles = (length - SUB) // rows
    upper = upper_ref[0] > 0
    row = lax.broadcasted_iota(jnp.int32, (rows, LANES), 0)
    for block in range(blocks):
        for c in range(tiles):
            start = (block * tiles + c) * LANES
            ratio = jnp.where(upper, message_ref[block, c * rows : (c + 1) * rows, :], 0.0)
            carry = jnp.where(upper, message_ref[block, tiles * rows + c : tiles * rows + c + 1, :], 0.0)
            peak = jnp.maximum(jnp.abs(ratio), carry)
            span = 1
            while span < rows:
                peak = jnp.maximum(peak, jnp.where(row >= span, pltpu.roll(peak, span, 0), 0.0))
                span *= 2
            out_ref[:, start : start + LANES] = ratio
            peak_ref[:, start : start + LANES] = peak


SMEM = pl.BlockSpec(memory_space=pltpu.SMEM)
VMEM = pl.BlockSpec(memory_space=pltpu.VMEM)


def f32(*shape):
    return jax.ShapeDtypeStruct(shape, jnp.float32)


def per_device(values, cloud_words, history_len, monitor_start, boundary_table, devices):
    rows, pixels = values.shape
    dates = boundary_table.shape[0]
    half = devices // 2
    late = dates // 2
    width = pixels // half
    length = width // LANES * rows + SUB
    groups = [list(range(half)), list(range(half, devices))]
    upward = [(i, i + half) for i in range(half)]
    design = design_table(dates)
    spread = spread_table(width, max(1, rows // SUB))

    def exchange(blocks):
        return lax.all_to_all(blocks, AXES, 0, 0, axis_index_groups=groups, tiled=True)

    step_message = pl.BlockSpec((half // STEPS, length, LANES), lambda i: (i, 0, 0))
    step_pixels = pl.BlockSpec((rows, pixels // STEPS), lambda i: (0, i))
    step_words = pl.BlockSpec((rows, pixels // WORD // STEPS), lambda i: (0, i))
    message = pl.pallas_call(
        pack_kernel,
        grid=(STEPS,),
        out_shape=f32(half, length, LANES),
        in_specs=[step_pixels, step_words],
        out_specs=step_message,
        name="pack",
    )(values, cloud_words)
    own = exchange(message)
    early = lax.ppermute(own[half - WINDOW // rows :], AXES, upward)
    history = design[:late]
    stats = pl.pallas_call(
        functools.partial(fit_kernel, rows=rows),
        out_shape=f32(2 * COLS, width),
        in_specs=[SMEM] + [VMEM] * 5,
        out_specs=VMEM,
        name="fit",
    )(
        history_len,
        own,
        spread,
        np.concatenate(split_table(outer_table(history)), axis=0),
        np.concatenate(split_table(history.T), axis=0),
        six_wide(history),
    )
    stats = lax.ppermute(stats, AXES, upward)
    message = pl.pallas_call(
        functools.partial(ratio_kernel, rows=rows),
        out_shape=f32(half, length, LANES),
        in_specs=[SMEM] + [VMEM] * 6,
        out_specs=VMEM,
        name="ratio",
    )(monitor_start, own, early, stats, spread, six_wide(design[late - WINDOW :]), boundary_table.reshape(1, dates))
    upper = (lax.axis_index(AXES) >= half).astype(jnp.int32).reshape(1)
    return pl.pallas_call(
        finish_kernel,
        grid=(STEPS,),
        out_shape=(f32(rows, pixels), f32(rows, pixels)),
        in_specs=[SMEM, step_message],
        out_specs=(step_pixels, step_pixels),
        name="finish",
    )(upper, exchange(message))


def solution(mesh):
    placed = (P(AXES, None), P(AXES, None), P(), P(), P())
    return jax.shard_map(
        functools.partial(per_device, devices=mesh.size),
        mesh=mesh,
        in_specs=placed,
        out_specs=(P(AXES, None), P(AXES, None)),
        check_vma=False,
    )
```

time: 92.2 us -> 75.6 us (0.82)
  waiting for transfers between devices: 32.9 us -> 18.4 us
  blocking collectives: 12.6 us -> 23.1 us
  starting transfers between devices: 23.6 us -> 14.4 us
  local copies, waits for them, and re-layouts: 7.33 us -> 1.74 us
  Pallas kernels: 13 us -> 15.4 us
    all_to_all x3 -> x1, waiting for transfers between devices: 30.7 us -> 16.8 us  [exchange(): lax.all_to_all(blocks, AXES, 0, 0, axis_index_groups=groups, tiled=True)]
    all_to_all x1, blocking collectives: 12.6 us -> 23.1 us  [exchange(): lax.all_to_all(blocks, AXES, 0, 0, axis_index_groups=groups, tiled=True)]
    all_to_all x3 -> x1, starting transfers between devices: 13.6 us -> 8.65 us  [exchange(): lax.all_to_all(blocks, AXES, 0, 0, axis_index_groups=groups, tiled=True)]
    ppermute x2 -> x1, starting transfers between devices: 8.75 us -> 4.51 us  [per_device(): early = lax.ppermute(own[half - WINDOW // rows:], AXES, upward)]
    reshape x4 -> x0, local copies, waits for them, and re-layouts: 3.18 us -> none  [the longest x1 2.31 us: per_device(): values.reshape(rows, half, width).transpose(1, 0, 2)]
    pallas_call x3 -> x4, Pallas kernels: 13 us -> 15.4 us  [the longest x1 4.18 us: per_device(): pl.pallas_call(functools.partial(fit_kernel, rows=rows), out_shape=f32(2...]
    all_to_all x2 -> x0, local copies, waits for them, and re-layouts: 1.64 us -> none  [exchange(): lax.all_to_all(blocks, AXES, 0, 0, axis_index_groups=groups, tiled=True)]
  transfers between devices with their start and end apart: 6 -> 3, of which waited for: 3 -> 2; matrix products, arithmetic and copies ran while one was open for 2% -> 0% of each run, Pallas kernels for 6% -> 6%
where the time goes in v2:
time: 75.6 us; the launch traced here: 75.1 us
  blocking collectives  23.1 us (31%)
  waiting for transfers between devices  18.4 us (24%)
  Pallas kernels  15.4 us (20%)
  starting transfers between devices  14.4 us (19%)
  between operations  1.97 us (3%)
  local copies, waits for them, and re-layouts  1.74 us (2%)
    all_to_all x1, blocking collectives, exchange(): lax.all_to_all(blocks, AXES, 0, 0, axis_index_groups=groups, tiled=True)  23.1 us
    all_to_all x1, waiting for transfers between devices, exchange(): lax.all_to_all(blocks, AXES, 0, 0, axis_index_groups=groups, tiled=True)  16.8 us
    all_to_all x1, starting transfers between devices, exchange(): lax.all_to_all(blocks, AXES, 0, 0, axis_index_groups=groups, tiled=True)  8.65 us
    ppermute x1, starting transfers between devices, per_device(): early = lax.ppermute(own[half - WINDOW // rows:], AXES, upward)  4.51 us
    pallas_call x1, Pallas kernels, per_device(): pl.pallas_call(functools.partial(fit_kernel, rows=rows), out_shape=f32(2...  4.18 us
    pallas_call x1, Pallas kernels, per_device(): pl.pallas_call(functools.partial(ratio_kernel, rows=rows), out_shape=f32(...  4.05 us
    pallas_call x1, Pallas kernels, per_device(): pl.pallas_call(finish_kernel, grid=(STEPS,), out_shape=(f32(rows, pixels)...  3.63 us
    pallas_call x1, Pallas kernels, per_device(): pl.pallas_call(pack_kernel, grid=(STEPS,), out_shape=f32(half, length, LA...  3.5 us
  transfers between devices with their start and end apart: 3, of which 2 were waited for; matrix products, arithmetic and copies ran while one was open for 0% of the time, Pallas kernels for 6%

profile of v2, /device:TPU:0, one launch (start us, length us, event | category | flops | bytes accessed | tf_op | source)
XLA Modules:
  0.0 75.1 jit_solution(14897451170112398933)
XLA Ops:
  0.6 3.5 %pack.1 = f32[16,136,128]{2,1,0:T(8,128)} custom-call(f32[16,16384]{1,0:T(8,128)} %values_ref.1, s32[16,512]{1,0:T(8,128)} %words_ref.1), custom_call_target="tpu_custom_call" | custom-call | tf_op jit(solution)/shard_map/pack/pallas_call | solution.py:256
  4.1 23.1 %all_to_all.10.message_ref = f32[16,136,128]{2,1,0:T(8,128)S(1)} all-to-all(f32[16,136,128]{2,1,0:T(8,128)} %pack.1), channel_id=1, replica_groups={{0,1,2,3,4,5,6,7,8,9,10,11,12,13,14,15},{16,17,18,19,20,21,22,23,24,25,..., dimensions={0} | all-to-all | bytes 2228224 | tf_op jit(solution)/shard_map/all_to_all | solution.py:251
  27.3 0.0 copy-start
  27.3 4.5 %collective-permute-start = (f32[4,136,128]{2,1,0:T(8,128)S(1)}, f32[4,136,128]{2,1,0:T(8,128)S(1)}, u32[]{:S(2)}, u32[]{:S(2)}) collective-permute-start(f32[4,136,128]{2,1,0:T(8,128)S(1)} %slice.4), channel_id=1, source_target_pairs={{0,16},{1,17},{2,18},{3,19},{4,20},{5,21},{6,22},{7,23},{8,24},{9,... | collective-permute-start | bytes 835592 | tf_op jit(solution)/shard_map/ppermute | solution.py:265
  32.5 0.0 copy-done
  32.5 4.2 %fit.1 = f32[16,1024]{1,0:T(8,128)} custom-call(s32[1]{0:T(128)S(6)} %copy.12.history_ref, f32[16,136,128]{2,1,0:T(8,128)} %copy-done, bf16[2,256,1024]{2,1,0:T(8,128)(2,1)} %constant.23.clone.spread_ref, bf16[120,256]{1,0:T(8,128)(2,1)} %constant.24.clone.outer_ref, bf16[24,256]{1,0:T(8,128)(2,1)} %constant.25.clone.turned_ref, ...), custom_call_target="tpu_custom_call" | custom-call | tf_op jit(solution)/shard_map/fit/pallas_call | solution.py:267
  36.7 1.3 %collective-permute-start.1 = (f32[16,1024]{1,0:T(8,128)}, f32[16,1024]{1,0:T(8,128)S(1)}, u32[]{:S(2)}, u32[]{:S(2)}) collective-permute-start(f32[16,1024]{1,0:T(8,128)} %fit.1), channel_id=1, source_target_pairs={{0,16},{1,17},{2,18},{3,19},{4,20},{5,21},{6,22},{7,23},{8,24},{9,... | collective-permute-start | bytes 196616 | tf_op jit(solution)/shard_map/ppermute | solution.py:281
  38.6 1.6 %collective-permute-done.1.stats_ref = f32[16,1024]{1,0:T(8,128)S(1)} collective-permute-done((f32[16,1024]{1,0:T(8,128)}, f32[16,1024]{1,0:T(8,128)S(1)}, u32[]{:S(2)}, u32[]{:S(2)}) %collective-permute-start.1) | collective-permute-done | bytes 65568 | tf_op jit(solution)/shard_map/ppermute | solution.py:281
  40.2 0.0 copy-start.3
  40.2 0.0 collective-permute-done.early_ref
  40.2 0.0 copy-start.2
  40.2 0.6 copy-done.3
  40.8 0.1 copy-done.2
  40.9 4.1 %ratio.1 = f32[16,136,128]{2,1,0:T(8,128)} custom-call(s32[1]{0:T(128)S(6)} %copy.13.start_ref, f32[16,136,128]{2,1,0:T(8,128)} %copy-done, f32[4,136,128]{2,1,0:T(8,128)} %copy-done.2, f32[16,1024]{1,0:T(8,128)} %copy-done.3, bf16[2,256,1024]{2,1,0:T(8,128)(2,1)} %constant.23.clone.spread_ref, bf16[320,48]{1,0:T(8,128)(2,1)} %constant.27.clone.design_ref, ...), custom_call_target="tpu_custom_call" | custom-call | tf_op jit(solution)/shard_map/ratio/pallas_call | solution.py:282
  44.9 8.6 %all-to-all-start.1 = ((f32[16,136,128]{2,1,0:T(8,128)}), f32[16,136,128]{2,1,0:T(8,128)S(1)}, u32[]{:S(2)}, u32[]{:S(2)}) async-start(f32[16,136,128]{2,1,0:T(8,128)} %ratio.1), calls=%async_computation.1 | async-start | bytes 2228224 | tf_op jit(solution)/shard_map/all_to_all | solution.py:251
  53.6 16.8 %all-to-all-done.1.message_ref = f32[16,136,128]{2,1,0:T(8,128)S(1)} async-done(((f32[16,136,128]{2,1,0:T(8,128)}), f32[16,136,128]{2,1,0:T(8,128)S(1)}, u32[]{:S(2)}, u32[]{:S(2)}) %all-to-all-start.1) | async-done | bytes 1114144 | tf_op jit(solution)/shard_map/all_to_all | solution.py:251
  70.4 0.0 copy-start.1
  70.4 1.0 %copy-done.1 = f32[16,136,128]{2,1,0:T(8,128)} copy-done((f32[16,136,128]{2,1,0:T(8,128)}, f32[16,136,128]{2,1,0:T(8,128)S(1)}, u32[]{:S(2)}) %copy-start.1) | copy-done | bytes 1114136
  71.4 3.6 %finish.1 = (f32[16,16384]{1,0:T(8,128)}, f32[16,16384]{1,0:T(8,128)}) custom-call(s32[1]{0:T(128)} %bitcast.upper_ref, f32[16,136,128]{2,1,0:T(8,128)} %copy-done.1), custom_call_target="tpu_custom_call" | custom-call | tf_op jit(solution)/shard_map/finish/pallas_call | solution.py:290
  (1 shorter events, 0.0 us)
Async XLA Ops:
  27.3 5.2 %copy-start = (f32[16,136,128]{2,1,0:T(8,128)}, f32[16,136,128]{2,1,0:T(8,128)S(1)}, u32[]{:S(2)}) copy-start(f32[16,136,128]{2,1,0:T(8,128)S(1)} %all_to_all.10.message_ref) | copy-start | bytes 3342340
  27.3 12.9 %collective-permute-start = (f32[4,136,128]{2,1,0:T(8,128)S(1)}, f32[4,136,128]{2,1,0:T(8,128)S(1)}, u32[]{:S(2)}, u32[]{:S(2)}) collective-permute-start(f32[4,136,128]{2,1,0:T(8,128)S(1)} %slice.4), channel_id=1, source_target_pairs={{0,16},{1,17},{2,18},{3,19},{4,20},{5,21},{6,22},{7,23},{8,24},{9,... | collective-permute-start | bytes 835592 | tf_op jit(solution)/shard_map/ppermute | solution.py:265
  36.7 3.5 %collective-permute-start.1 = (f32[16,1024]{1,0:T(8,128)}, f32[16,1024]{1,0:T(8,128)S(1)}, u32[]{:S(2)}, u32[]{:S(2)}) collective-permute-start(f32[16,1024]{1,0:T(8,128)} %fit.1), channel_id=1, source_target_pairs={{0,16},{1,17},{2,18},{3,19},{4,20},{5,21},{6,22},{7,23},{8,24},{9,... | collective-permute-start | bytes 196616 | tf_op jit(solution)/shard_map/ppermute | solution.py:281
  40.2 0.6 copy-start.3
  40.2 0.7 copy-start.2
  44.9 25.5 %all-to-all-start.1 = ((f32[16,136,128]{2,1,0:T(8,128)}), f32[16,136,128]{2,1,0:T(8,128)S(1)}, u32[]{:S(2)}, u32[]{:S(2)}) async-start(f32[16,136,128]{2,1,0:T(8,128)} %ratio.1), calls=%async_computation.1 | async-start | bytes 2228224 | tf_op jit(solution)/shard_map/all_to_all | solution.py:251
  70.4 1.0 %copy-start.1 = (f32[16,136,128]{2,1,0:T(8,128)}, f32[16,136,128]{2,1,0:T(8,128)S(1)}, u32[]{:S(2)}) copy-start(f32[16,136,128]{2,1,0:T(8,128)S(1)} %all-to-all-done.1.message_ref) | copy-start | bytes 3342340

commit v3 on v2

--- a/solution.py
+++ b/solution.py
@@ -153,10 +153,12 @@
         message_ref[block, tiles * rows :, :] = riding.astype(jnp.float32)
 
 
-def fit_kernel(history_ref, message_ref, spread_ref, outer_ref, turned_ref, design_ref, stats_ref, *, rows):
+def fit_kernel(history_ref, message_ref, spread_ref, outer_ref, turned_ref, design_ref, stats_ref, values_ref, clear_ref, *, rows):
     message = message_ref[...]
     clear = read_clear(message, rows, spread_ref)
     values = read_values(message, rows)
+    values_ref[...] = values
+    clear_ref[...] = clear
     day = lax.broadcasted_iota(jnp.int32, clear.shape, 0)
     weight = jnp.where(day < history_ref[0], clear, 0.0)
     tripled = jnp.dot(outer_ref[...], weight.astype(jnp.bfloat16), preferred_element_type=jnp.float32)
@@ -171,21 +173,25 @@
         lambda i, j: normal[i * (i + 1) // 2 + j][None, :],
         lambda i: target[i][None, :],
     )
-    for i in range(COLS):
-        stats_ref[i : i + 1, :] = solved[i]
-    resid = weight * (values - fit_dot(design_ref, stats_ref[0:COLS, :]))
+    resid = weight * (values - fit_dot(design_ref, jnp.concatenate(solved, axis=0)))
     squares = jnp.sum(resid * resid, axis=0, keepdims=True)
     count = normal[0:1, :]
     sigma = jnp.sqrt(squares / (count - COLS) + 1e-06)
-    stats_ref[COLS : COLS + 1, :] = 1.0 / (sigma * jnp.sqrt(count))
-    stats_ref[COLS + 1 :, :] = jnp.zeros_like(stats_ref[COLS + 1 :, :])
-
-
-def ratio_kernel(start_ref, message_ref, early_ref, stats_ref, spread_ref, design_ref, bounds_ref, out_ref, *, rows):
-    message = jnp.concatenate([early_ref[...], message_ref[...]], axis=0)
-    clear = read_clear(message, rows, spread_ref)
-    values = read_values(message, rows)
-    moving = clear * (values - fit_dot(design_ref, stats_ref[0:COLS, :]))
+    tiles = count.shape[1] // LANES
+    for i, stat in enumerate(solved + [1.0 / (sigma * jnp.sqrt(count))]):
+        for c in range(tiles):
+            stats_ref[i * tiles + c : i * tiles + c + 1, :] = stat[:, c * LANES : (c + 1) * LANES]
+
+
+def ratio_kernel(start_ref, values_ref, clear_ref, early_ref, stats_ref, spread_ref, design_ref, bounds_ref, out_ref, *, rows):
+    tiles = stats_ref.shape[0] // (COLS + 1)
+    early = early_ref[...]
+    clear = jnp.concatenate([read_clear(early, rows, spread_ref), clear_ref[...]], axis=0)
+    values = jnp.concatenate([read_values(early, rows), values_ref[...]], axis=0)
+    stat_rows = [stats_ref[pl.ds(c, COLS + 1, stride=tiles), :] for c in range(tiles)]
+    coeffs = jnp.concatenate([stat[:COLS] for stat in stat_rows], axis=1)
+    scale = jnp.concatenate([stat[COLS:] for stat in stat_rows], axis=1)
+    moving = clear * (values - fit_dot(design_ref, coeffs))
     span = 1
     while span < WINDOW:
         moving = moving + pltpu.roll(moving, span, 0)
@@ -194,9 +200,8 @@
     day = late + lax.broadcasted_iota(jnp.int32, (SUB, late), 1)
     bounds = jnp.broadcast_to(bounds_ref[:, late:].astype(jnp.float32), (SUB, late)) * 0.001
     factor = jnp.transpose(jnp.where(day >= start_ref[0], 1.0 / bounds, 0.0))[:, 0:1]
-    ratio = moving[WINDOW:] * stats_ref[COLS : COLS + 1, :] * factor
+    ratio = moving[WINDOW:] * scale * factor
     blocks = out_ref.shape[0]
-    tiles = ratio.shape[1] // LANES
     running = jnp.zeros((1, ratio.shape[1]), jnp.float32)
     for block in range(blocks):
         part = ratio[block * rows : (block + 1) * rows]
@@ -208,16 +213,18 @@
 
 
 def finish_kernel(upper_ref, message_ref, out_ref, peak_ref):
-    blocks, length, _ = message_ref.shape
-    rows = out_ref.shape[0]
+    _, length, _ = message_ref.shape
+    rows, lanes = out_ref.shape
     tiles = (length - SUB) // rows
+    blocks = lanes // (tiles * LANES)
+    first = pl.program_id(0) * blocks
     upper = upper_ref[0] > 0
     row = lax.broadcasted_iota(jnp.int32, (rows, LANES), 0)
     for block in range(blocks):
         for c in range(tiles):
             start = (block * tiles + c) * LANES
-            ratio = jnp.where(upper, message_ref[block, c * rows : (c + 1) * rows, :], 0.0)
-            carry = jnp.where(upper, message_ref[block, tiles * rows + c : tiles * rows + c + 1, :], 0.0)
+            ratio = jnp.where(upper, message_ref[first + block, c * rows : (c + 1) * rows, :], 0.0)
+            carry = jnp.where(upper, message_ref[first + block, tiles * rows + c : tiles * rows + c + 1, :], 0.0)
             peak = jnp.maximum(jnp.abs(ratio), carry)
             span = 1
             while span < rows:
@@ -228,6 +235,7 @@
 
 
 SMEM = pl.BlockSpec(memory_space=pltpu.SMEM)
+GRANT = pltpu.CompilerParams(vmem_limit_bytes=24 << 20)
 VMEM = pl.BlockSpec(memory_space=pltpu.VMEM)
 
 
@@ -259,16 +267,18 @@
         out_shape=f32(half, length, LANES),
         in_specs=[step_pixels, step_words],
         out_specs=step_message,
+        compiler_params=GRANT,
         name="pack",
     )(values, cloud_words)
     own = exchange(message)
     early = lax.ppermute(own[half - WINDOW // rows :], AXES, upward)
     history = design[:late]
-    stats = pl.pallas_call(
+    stats, values, clear = pl.pallas_call(
         functools.partial(fit_kernel, rows=rows),
-        out_shape=f32(2 * COLS, width),
+        out_shape=(f32((COLS + 1) * (width // LANES), LANES), f32(late, width), f32(late, width)),
         in_specs=[SMEM] + [VMEM] * 5,
-        out_specs=VMEM,
+        out_specs=(VMEM, VMEM, VMEM),
+        compiler_params=GRANT,
         name="fit",
     )(
         history_len,
@@ -282,17 +292,19 @@
     message = pl.pallas_call(
         functools.partial(ratio_kernel, rows=rows),
         out_shape=f32(half, length, LANES),
-        in_specs=[SMEM] + [VMEM] * 6,
+        in_specs=[SMEM] + [VMEM] * 7,
         out_specs=VMEM,
+        compiler_params=GRANT,
         name="ratio",
-    )(monitor_start, own, early, stats, spread, six_wide(design[late - WINDOW :]), boundary_table.reshape(1, dates))
+    )(monitor_start, values, clear, early, stats, spread, six_wide(design[late - WINDOW :]), boundary_table.reshape(1, dates))
     upper = (lax.axis_index(AXES) >= half).astype(jnp.int32).reshape(1)
     return pl.pallas_call(
         finish_kernel,
         grid=(STEPS,),
         out_shape=(f32(rows, pixels), f32(rows, pixels)),
-        in_specs=[SMEM, step_message],
+        in_specs=[SMEM, VMEM],
         out_specs=(step_pixels, step_pixels),
+        compiler_params=GRANT,
         name="finish",
     )(upper, exchange(message))
 

time: 75.6 us -> 67.8 us (0.90)
  Pallas kernels: 15.4 us -> 6.61 us
    pallas_call x1, Pallas kernels: 3.5 us -> 0.48 us  [per_device(): pl.pallas_call(pack_kernel, grid=(STEPS,), out_shape=f32(half, length, LA...]
    pallas_call x1, Pallas kernels: 4.18 us -> 1.97 us  [per_device(): pl.pallas_call(functools.partial(fit_kernel, rows=rows), out_shape=(f32((...]
    pallas_call x1, Pallas kernels: 4.05 us -> 2.29 us  [per_device(): pl.pallas_call(functools.partial(ratio_kernel, rows=rows), out_shape=f32(...]
    pallas_call x1, Pallas kernels: 3.63 us -> 1.87 us  [per_device(): pl.pallas_call(finish_kernel, grid=(STEPS,), out_shape=(f32(rows, pixels)...]
    unnamed x8 -> x16, local copies, waits for them, and re-layouts: 1.72 us -> 2.02 us
  transfers between devices with their start and end apart: 3 -> 3, of which waited for: 2 -> 2; matrix products, arithmetic and copies ran while one was open for 0% -> 0% of each run, Pallas kernels for 6% -> 3%
where the time goes in v3:
time: 67.8 us; the launch traced here: 67.4 us
  blocking collectives  23.1 us (34%)
  waiting for transfers between devices  18.8 us (28%)
  starting transfers between devices  14.8 us (22%)
  Pallas kernels  6.61 us (10%)
  between operations  2.07 us (3%)
  local copies, waits for them, and re-layouts  2.03 us (3%)
    all_to_all x1, blocking collectives, exchange(): lax.all_to_all(blocks, AXES, 0, 0, axis_index_groups=groups, tiled=True)  23.1 us
    all_to_all x1, waiting for transfers between devices, exchange(): lax.all_to_all(blocks, AXES, 0, 0, axis_index_groups=groups, tiled=True)  16.8 us
    all_to_all x1, starting transfers between devices, exchange(): lax.all_to_all(blocks, AXES, 0, 0, axis_index_groups=groups, tiled=True)  9 us
    ppermute x1, starting transfers between devices, per_device(): early = lax.ppermute(own[half - WINDOW // rows:], AXES, upward)  4.51 us
    pallas_call x1, Pallas kernels, per_device(): pl.pallas_call(functools.partial(ratio_kernel, rows=rows), out_shape=f32(...  2.29 us
    unnamed x16, local copies, waits for them, and re-layouts  2.02 us
    ppermute x1, waiting for transfers between devices, per_device(): stats = lax.ppermute(stats, AXES, upward)  2.01 us
    pallas_call x1, Pallas kernels, per_device(): pl.pallas_call(functools.partial(fit_kernel, rows=rows), out_shape=(f32((...  1.97 us
  transfers between devices with their start and end apart: 3, of which 2 were waited for; matrix products, arithmetic and copies ran while one was open for 0% of the time, Pallas kernels for 3%

profile of v3, /device:TPU:0, one launch (start us, length us, event | category | flops | bytes accessed | tf_op | source)
XLA Modules:
  0.0 67.4 jit_solution(1467835375949287474)
XLA Ops:
  0.6 0.0 copy-start.1
  0.6 1.2 %copy-done.1 = f32[16,16384]{1,0:T(8,128)S(1)} copy-done((f32[16,16384]{1,0:T(8,128)S(1)}, f32[16,16384]{1,0:T(8,128)}, u32[]{:S(2)}) %copy-start.1) | copy-done | bytes 1048600
  1.9 0.0 copy-start.5
  1.9 0.8 %copy-done.5 = s32[16,512]{1,0:T(8,128)S(1)} copy-done((s32[16,512]{1,0:T(8,128)S(1)}, s32[16,512]{1,0:T(8,128)}, u32[]{:S(2)}) %copy-start.5) | copy-done | bytes 32792
  2.6 0.5 pack.1
  3.1 0.0 copy-start
  3.1 0.0 copy-start.3
  3.1 0.0 copy-start.4
  3.1 0.0 copy-start.6
  3.1 23.1 %all_to_all.10.message_ref = f32[16,136,128]{2,1,0:T(8,128)S(1)} all-to-all(f32[16,136,128]{2,1,0:T(8,128)S(1)} %pack.1), channel_id=1, replica_groups={{0,1,2,3,4,5,6,7,8,9,10,11,12,13,14,15},{16,17,18,19,20,21,22,23,24,25,..., dimensions={0} | all-to-all | bytes 2228224 | tf_op jit(solution)/shard_map/all_to_all | solution.py:259
  26.3 4.5 %collective-permute-start = (f32[4,136,128]{2,1,0:T(8,128)S(1)}, f32[4,136,128]{2,1,0:T(8,128)S(1)}, u32[]{:S(2)}, u32[]{:S(2)}) collective-permute-start(f32[4,136,128]{2,1,0:T(8,128)S(1)} %slice.4), channel_id=1, source_target_pairs={{0,16},{1,17},{2,18},{3,19},{4,20},{5,21},{6,22},{7,23},{8,24},{9,... | collective-permute-start | bytes 835592 | tf_op jit(solution)/shard_map/ppermute | solution.py:274
  31.4 0.0 copy-done
  31.4 0.0 copy-done.3
  31.4 0.0 copy-done.4
  31.4 0.0 copy-done.6
  31.5 0.0 copy-start.2
  31.5 0.0 copy-start.7
  31.5 2.0 %fit.1 = (f32[72,128]{1,0:T(8,128)S(1)}, f32[256,1024]{1,0:T(8,128)S(1)}, f32[256,1024]{1,0:T(8,128)S(1)}) custom-call(s32[1]{0:T(128)S(6)} %copy.12.history_ref, f32[16,136,128]{2,1,0:T(8,128)S(1)} %all_to_all.10.message_ref, bf16[2,256,1024]{2,1,0:T(8,128)(2,1)S(1)} %copy-done, bf16[120,256]{1,0:T(8,128)(2,1)S(1)} %copy-done.4, ...), custom_call_target="tpu_custom_call" | custom-call | tf_op jit(solution)/shard_map/fit/pallas_call | solution.py:276
  33.5 1.3 %collective-permute-start.1 = (f32[72,128]{1,0:T(8,128)S(1)}, f32[72,128]{1,0:T(8,128)S(1)}, u32[]{:S(2)}, u32[]{:S(2)}) collective-permute-start(f32[72,128]{1,0:T(8,128)S(1)} %get-tuple-element.7), channel_id=1, source_target_pairs={{0,16},{1,17},{2,18},{3,19},{4,20},{5,21},{6,22},{7,23},{8,24},{9,... | collective-permute-start | bytes 110600 | tf_op jit(solution)/shard_map/ppermute | solution.py:291
  35.4 2.0 %collective-permute-done.1.stats_ref = f32[72,128]{1,0:T(8,128)S(1)} collective-permute-done((f32[72,128]{1,0:T(8,128)S(1)}, f32[72,128]{1,0:T(8,128)S(1)}, u32[]{:S(2)}, u32[]{:S(2)}) %collective-permute-start.1) | collective-permute-done | bytes 36896 | tf_op jit(solution)/shard_map/ppermute | solution.py:291
  37.4 0.0 collective-permute-done.early_ref
  37.4 0.0 copy-done.2
  37.4 0.0 copy-done.7
  37.4 2.3 %ratio.1 = f32[16,136,128]{2,1,0:T(8,128)} custom-call(s32[1]{0:T(128)S(6)} %copy.13.start_ref, f32[256,1024]{1,0:T(8,128)S(1)} %get-tuple-element.5.values_ref, f32[256,1024]{1,0:T(8,128)S(1)} %get-tuple-element.6.clear_ref, f32[4,136,128]{2,1,0:T(8,128)S(1)} %collective-permute-done.early_ref, f32[72,128]{1,0:T(8,128)S(1)} %collective-permute-done.1.stats_ref, ...), custom_call_target="tpu_custom_call" | custom-call | tf_op jit(solution)/shard_map/ratio/pallas_call | solution.py:292
  39.7 9.0 %all-to-all-start.1 = ((f32[16,136,128]{2,1,0:T(8,128)}), f32[16,136,128]{2,1,0:T(8,128)S(1)}, u32[]{:S(2)}, u32[]{:S(2)}) async-start(f32[16,136,128]{2,1,0:T(8,128)} %ratio.1), calls=%async_computation.1 | async-start | bytes 2228224 | tf_op jit(solution)/shard_map/all_to_all | solution.py:259
  48.7 16.8 %all-to-all-done.1.message_ref = f32[16,136,128]{2,1,0:T(8,128)S(1)} async-done(((f32[16,136,128]{2,1,0:T(8,128)}), f32[16,136,128]{2,1,0:T(8,128)S(1)}, u32[]{:S(2)}, u32[]{:S(2)}) %all-to-all-start.1) | async-done | bytes 1114144 | tf_op jit(solution)/shard_map/all_to_all | solution.py:259
  65.6 1.9 %finish.1 = (f32[16,16384]{1,0:T(8,128)}, f32[16,16384]{1,0:T(8,128)}) custom-call(s32[1]{0:T(128)} %bitcast.upper_ref, f32[16,136,128]{2,1,0:T(8,128)S(1)} %all-to-all-done.1.message_ref), custom_call_target="tpu_custom_call" | custom-call | tf_op jit(solution)/shard_map/finish/pallas_call | solution.py:301
  (1 shorter events, 0.0 us)
Async XLA Ops:
  0.6 1.2 %copy-start.1 = (f32[16,16384]{1,0:T(8,128)S(1)}, f32[16,16384]{1,0:T(8,128)}, u32[]{:S(2)}) copy-start(f32[16,16384]{1,0:T(8,128)} %values_ref.1) | copy-start | bytes 3145732
  1.9 0.8 %copy-start.5 = (s32[16,512]{1,0:T(8,128)S(1)}, s32[16,512]{1,0:T(8,128)}, u32[]{:S(2)}) copy-start(s32[16,512]{1,0:T(8,128)} %words_ref.1) | copy-start | bytes 98308
  3.1 28.3 %copy-start = (bf16[2,256,1024]{2,1,0:T(8,128)(2,1)S(1)}, bf16[2,256,1024]{2,1,0:T(8,128)(2,1)}, u32[]{:S(2)}) copy-start(bf16[2,256,1024]{2,1,0:T(8,128)(2,1)} %constant.23.clone.spread_ref) | copy-start | bytes 3145732
  3.1 28.3 %copy-start.3 = (bf16[256,48]{1,0:T(8,128)(2,1)S(1)}, bf16[256,48]{1,0:T(8,128)(2,1)}, u32[]{:S(2)}) copy-start(bf16[256,48]{1,0:T(8,128)(2,1)} %constant.26.clone.design_ref) | copy-start | bytes 73732
  3.1 28.3 %copy-start.4 = (bf16[120,256]{1,0:T(8,128)(2,1)S(1)}, bf16[120,256]{1,0:T(8,128)(2,1)}, u32[]{:S(2)}) copy-start(bf16[120,256]{1,0:T(8,128)(2,1)} %constant.24.clone.outer_ref) | copy-start | bytes 184324
  3.1 28.3 %copy-start.6 = (bf16[24,256]{1,0:T(8,128)(2,1)S(1)}, bf16[24,256]{1,0:T(8,128)(2,1)}, u32[]{:S(2)}) copy-start(bf16[24,256]{1,0:T(8,128)(2,1)} %constant.25.clone.turned_ref) | copy-start | bytes 36868
  26.3 11.2 %collective-permute-start = (f32[4,136,128]{2,1,0:T(8,128)S(1)}, f32[4,136,128]{2,1,0:T(8,128)S(1)}, u32[]{:S(2)}, u32[]{:S(2)}) collective-permute-start(f32[4,136,128]{2,1,0:T(8,128)S(1)} %slice.4), channel_id=1, source_target_pairs={{0,16},{1,17},{2,18},{3,19},{4,20},{5,21},{6,22},{7,23},{8,24},{9,... | collective-permute-start | bytes 835592 | tf_op jit(solution)/shard_map/ppermute | solution.py:274
  31.5 6.0 %copy-start.2 = (bf16[320,48]{1,0:T(8,128)(2,1)S(1)}, bf16[320,48]{1,0:T(8,128)(2,1)}, u32[]{:S(2)}) copy-start(bf16[320,48]{1,0:T(8,128)(2,1)} %constant.27.clone.design_ref) | copy-start | bytes 92164
  31.5 6.0 %copy-start.7 = (s32[512]{0:T(512)S(1)}, s32[512]{0:T(512)}, u32[]{:S(2)}) copy-start(s32[512]{0:T(512)} %param.14) | copy-start | bytes 6148
  33.5 4.0 %collective-permute-start.1 = (f32[72,128]{1,0:T(8,128)S(1)}, f32[72,128]{1,0:T(8,128)S(1)}, u32[]{:S(2)}, u32[]{:S(2)}) collective-permute-start(f32[72,128]{1,0:T(8,128)S(1)} %get-tuple-element.7), channel_id=1, source_target_pairs={{0,16},{1,17},{2,18},{3,19},{4,20},{5,21},{6,22},{7,23},{8,24},{9,... | collective-permute-start | bytes 110600 | tf_op jit(solution)/shard_map/ppermute | solution.py:291
  39.7 25.9 %all-to-all-start.1 = ((f32[16,136,128]{2,1,0:T(8,128)}), f32[16,136,128]{2,1,0:T(8,128)S(1)}, u32[]{:S(2)}, u32[]{:S(2)}) async-start(f32[16,136,128]{2,1,0:T(8,128)} %ratio.1), calls=%async_computation.1 | async-start | bytes 2228224 | tf_op jit(solution)/shard_map/all_to_all | solution.py:259
